TPU v7x, 16 devices: a whole 2x2x2 slice. The times are simulated.
16 devices in a mesh: dz: 2 (over z), dy: 2 (over y), dx: 4 (over x, core).
Axes of the slice: x: 2, y: 2, z: 2, core: 2. Of those that a mesh axis runs over, the one named last changes fastest.
Arguments:
- x: bfloat16 [65536, 1024], P(('dx', 'dy', 'dz'))
- g: bfloat16 [65536, 1024], P(('dx', 'dy', 'dz'))
- w1: bfloat16 [1024, 4096], replicated
- w2: bfloat16 [4096, 1024], replicated
- w3: bfloat16 [1024, 4096], replicated
- w4: bfloat16 [4096, 1024], replicated
- m1: float32 [1024, 4096], P(('dx', 'dy', 'dz'))
- m2: float32 [4096, 1024], P(('dx', 'dy', 'dz'))
- m3: float32 [1024, 4096], P(('dx', 'dy', 'dz'))
- m4: float32 [4096, 1024], P(('dx', 'dy', 'dz'))
Outputs:
- output 1: bfloat16 [65536, 1024], P(('dx', 'dy', 'dz'))
- output 2: bfloat16 [1024, 4096], replicated
- output 3: bfloat16 [4096, 1024], replicated
- output 4: bfloat16 [1024, 4096], replicated
- output 5: bfloat16 [4096, 1024], replicated
- output 6: float32 [1024, 4096], P(('dx', 'dy', 'dz'))
- output 7: float32 [4096, 1024], P(('dx', 'dy', 'dz'))
- output 8: float32 [1024, 4096], P(('dx', 'dy', 'dz'))
- output 9: float32 [4096, 1024], P(('dx', 'dy', 'dz'))
All inputs are finite; a program needn't handle non-finite values.
Results may differ from a plain program's by a relative error of at most 0.0121176.
Values are sent between devices in bfloat16 or wider.
A program may use at most 1 GiB of HBM per device.

v0:
```python
import jax
import jax.numpy as jnp
from jax import lax
from jax.sharding import PartitionSpec as P

LR = 0.0005
MU = 0.9
DATA = ("dx", "dy", "dz")


def _gelu(z):
    return jax.nn.gelu(z, approximate=True)


def _gelu_grad(z, dh):
    return jax.vjp(_gelu, z.astype(jnp.float32))[1](dh.astype(jnp.float32))[0]


def solution(mesh):
    ndy, ndz = mesh.shape["dy"], mesh.shape["dz"]
    n = mesh.shape["dx"] * ndy * ndz
    f32, bf = jnp.float32, jnp.bfloat16

    def reduce_scatter(s):
        for ax in DATA:
            s = lax.psum_scatter(s, ax, scatter_dimension=0, tiled=True)
        return s

    def all_gather(w):
        for ax in reversed(DATA):
            w = lax.all_gather(w, ax, axis=0, tiled=True)
        return w

    def update(w, m, s):
        idx = (lax.axis_index("dx") * ndy + lax.axis_index("dy")) * ndz + lax.axis_index("dz")
        rows = m.shape[0]
        w_loc = lax.dynamic_slice_in_dim(w, idx * rows, rows, 0).astype(f32)
        m_new = MU * m + s / n
        return all_gather((w_loc - LR * m_new).astype(bf)), m_new

    def local(x, g, w1, w2, w3, w4, m1, m2, m3, m4):
        z1 = jnp.dot(x, w1, preferred_element_type=f32).astype(bf)
        h1 = _gelu(z1.astype(f32)).astype(bf)
        h2 = (jnp.dot(h1, w2, preferred_element_type=f32) + x.astype(f32)).astype(bf)
        z3 = jnp.dot(h2, w3, preferred_element_type=f32).astype(bf)
        h3 = _gelu(z3.astype(f32)).astype(bf)
        s4 = reduce_scatter(jnp.dot(h3.T, g, preferred_element_type=f32))
        dh3 = jnp.dot(g, w4.T, preferred_element_type=f32).astype(bf)
        dz3 = _gelu_grad(z3, dh3).astype(bf)
        s3 = reduce_scatter(jnp.dot(h2.T, dz3, preferred_element_type=f32))
        dh2 = (jnp.dot(dz3, w3.T, preferred_element_type=f32) + g.astype(f32)).astype(bf)
        s2 = reduce_scatter(jnp.dot(h1.T, dh2, preferred_element_type=f32))
        dh1 = jnp.dot(dh2, w2.T, preferred_element_type=f32).astype(bf)
        dz1 = _gelu_grad(z1, dh1).astype(bf)
        s1 = reduce_scatter(jnp.dot(x.T, dz1, preferred_element_type=f32))
        dx = (jnp.dot(dz1, w1.T, preferred_element_type=f32) + dh2.astype(f32)).astype(bf)
        w4n, m4n = update(w4, m4, s4)
        w3n, m3n = update(w3, m3, s3)
        w2n, m2n = update(w2, m2, s2)
        w1n, m1n = update(w1, m1, s1)
        return (dx, w1n, w2n, w3n, w4n, m1n, m2n, m3n, m4n)

    row, rep = P(DATA, None), P()
    return jax.shard_map(local, mesh=mesh,
                         in_specs=(row, row, rep, rep, rep, rep, row, row, row, row),
                         out_specs=(row, rep, rep, rep, rep, row, row, row, row),
                         check_vma=False)
```

profile of v0, /device:TPU:0, one launch (start us, length us, event | category | flops | bytes accessed | tf_op | source)
XLA Modules:
  0.0 1529.7 jit_solution(1673831419857198592)
XLA Ops:
  7.2 43.0 %convolution_convert_fusion.1 = bf16[4096,4096]{1,0:T(8,128)(2,1)} fusion(bf16[4096,1024]{1,0:T(8,128)(2,1)} %param.10, bf16[1024,4096]{1,0:T(8,128)(2,1)} %param.12), kind=kOutput, calls=%fused_computation.36 | convolution fusion | flops 34376515584 | bytes 50331648 | tf_op jit(solution)/shard_map/dot_general | solution.py:42
  50.2 50.1 %add_convert_fusion.2 = bf16[4096,1024]{1,0:T(8,128)(2,1)} fusion(bf16[4096,1024]{1,0:T(8,128)(2,1)} %param.10, bf16[4096,1024]{1,0:T(8,128)(2,1)} %param.13, bf16[4096,4096]{1,0:T(8,128)(2,1)} %convolution_convert_fusion.1), kind=kOutput, calls=%fused_computation.39 | convolution fusion | flops 34540093440 | bytes 58720256 | tf_op jit(solution)/shard_map/dot_general | solution.py:44
  100.3 43.2 %convolution_convert_fusion = bf16[4096,4096]{1,0:T(8,128)(2,1)} fusion(bf16[4096,1024]{1,0:T(8,128)(2,1)} %add_convert_fusion.2, bf16[1024,4096]{1,0:T(8,128)(2,1)} %param.14), kind=kOutput, calls=%fused_computation.35 | convolution fusion | flops 34376515584 | bytes 50331648 | tf_op jit(solution)/shard_map/dot_general | solution.py:45
  143.4 55.5 %fusion.22 = f32[4096,1024]{1,0:T(8,128)} fusion(bf16[4096,1024]{1,0:T(8,128)(2,1)} %param.11, bf16[4096,4096]{1,0:T(8,128)(2,1)} %convolution_convert_fusion), kind=kOutput, calls=%fused_computation.34 | convolution fusion | flops 34527510528 | bytes 58720256 | tf_op jit(solution)/shard_map/dot_general | solution.py:47
  199.1 85.2 %fusion.4 = bf16[4096,4096]{1,0:T(8,128)(2,1)} fusion(bf16[4096,4096]{1,0:T(8,128)(2,1)} %convolution_convert_fusion, bf16[4096,1024]{1,0:T(8,128)(2,1)} %param.11, bf16[4096,1024]{1,0:T(8,128)(2,1)} %param.15), kind=kOutput, calls=%fused_computation.16 | convolution fusion | flops 34745614336 | bytes 83886080 | tf_op jit(solution)/shard_map/dot_general | solution.py:48
  284.2 42.7 %fusion.31 = f32[1024,4096]{1,0:T(8,128)} fusion(bf16[4096,1024]{1,0:T(8,128)(2,1)S(1)} %copy-done.2, bf16[4096,4096]{1,0:T(8,128)(2,1)} %fusion.4), kind=kOutput, calls=%fused_computation.56 | convolution fusion | flops 34359738368 | bytes 58720256 | tf_op jit(solution)/shard_map/dot_general | solution.py:50
  327.0 42.9 %add_convert_fusion.1 = bf16[4096,1024]{1,0:T(8,128)(2,1)} fusion(bf16[4096,1024]{1,0:T(8,128)(2,1)} %param.11, bf16[4096,4096]{1,0:T(8,128)(2,1)} %fusion.4, bf16[1024,4096]{1,0:T(8,128)(2,1)} %param.14), kind=kOutput, calls=%fused_computation.38 | convolution fusion | flops 34372321280 | bytes 58720256 | tf_op jit(solution)/shard_map/dot_general | solution.py:51
  369.9 55.5 %fusion.28 = f32[4096,1024]{1,0:T(8,128)} fusion(bf16[4096,1024]{1,0:T(8,128)(2,1)} %add_convert_fusion.1, bf16[4096,4096]{1,0:T(8,128)(2,1)} %convolution_convert_fusion.1), kind=kOutput, calls=%fused_computation.55 | convolution fusion | flops 34527510528 | bytes 58720256 | tf_op jit(solution)/shard_map/dot_general | solution.py:52
  425.5 85.2 %fusion.7 = bf16[4096,4096]{1,0:T(8,128)(2,1)} fusion(bf16[4096,4096]{1,0:T(8,128)(2,1)} %convolution_convert_fusion.1, bf16[4096,1024]{1,0:T(8,128)(2,1)} %add_convert_fusion.1, bf16[4096,1024]{1,0:T(8,128)(2,1)} %param.13), kind=kOutput, calls=%fused_computation.19 | convolution fusion | flops 34745614336 | bytes 83886080 | tf_op jit(solution)/shard_map/dot_general | solution.py:53
  510.7 42.1 %convolution_bitcast_fusion = f32[1024,4096]{0,1:T(8,128)} fusion(bf16[4096,4096]{1,0:T(8,128)(2,1)} %fusion.7, bf16[4096,1024]{1,0:T(8,128)(2,1)S(1)} %copy-done.1), kind=kOutput, calls=%fused_computation.40 | convolution fusion | flops 34359738368 | bytes 58720256 | tf_op jit(solution)/shard_map/dot_general | solution.py:55
  554.0 19.6 %reduce-scatter.21.cloned.1.call-done = f32[1024,1024]{1,0:T(8,128)} async-done(((f32[4096,1024]{1,0:T(8,128)}), f32[1024,1024]{1,0:T(8,128)}) %reduce-scatter.21.cloned.1.call-update) | async-done | bytes 4194320 | tf_op jit(solution)/shard_map/reduce_scatter | solution.py:26
  573.7 122.9 %reduce-scatter.17.cloned.1.call-done = f32[256,4096]{0,1:T(8,128)} async-done(((f32[1024,4096]{0,1:T(8,128)}), f32[256,4096]{0,1:T(8,128)}) %reduce-scatter.17.cloned.1.call-update) | async-done | bytes 4194320 | tf_op jit(solution)/shard_map/reduce_scatter | solution.py:26
  696.7 54.5 %reduce-scatter.33.cloned.1.call-done = f32[512,1024]{1,0:T(8,128)} async-done(((f32[1024,1024]{1,0:T(8,128)}), f32[512,1024]{1,0:T(8,128)}) %reduce-scatter.33.cloned.1.call-update) | async-done | bytes 2097168 | tf_op jit(solution)/shard_map/reduce_scatter | solution.py:26
  751.3 54.5 %reduce-scatter.29.cloned.1.call-done = f32[128,4096]{1,0:T(8,128)} async-done(((f32[256,4096]{1,0:T(8,128)}), f32[128,4096]{1,0:T(8,128)}) %reduce-scatter.29.cloned.1.call-update) | async-done | bytes 2097168 | tf_op jit(solution)/shard_map/reduce_scatter | solution.py:26
  805.9 54.6 %reduce-scatter.23.cloned.1.call-done = f32[512,1024]{1,0:T(8,128)} async-done(((f32[1024,1024]{1,0:T(8,128)}), f32[512,1024]{1,0:T(8,128)}) %reduce-scatter.23.cloned.1.call-update) | async-done | bytes 2097168 | tf_op jit(solution)/shard_map/reduce_scatter | solution.py:26
  860.6 54.6 %reduce-scatter.19.cloned.1.call-done = f32[128,4096]{0,1:T(8,128)} async-done(((f32[256,4096]{0,1:T(8,128)}), f32[128,4096]{0,1:T(8,128)}) %reduce-scatter.19.cloned.1.call-update) | async-done | bytes 2097168 | tf_op jit(solution)/shard_map/reduce_scatter | solution.py:26
  921.7 25.7 %reduce-scatter.35.cloned.1.call-done = f32[256,1024]{1,0:T(8,128)} async-done(((f32[512,1024]{1,0:T(8,128)}), f32[256,1024]{1,0:T(8,128)}) %reduce-scatter.35.cloned.1.call-update) | async-done | bytes 1048592 | tf_op jit(solution)/shard_map/reduce_scatter | solution.py:26
  950.7 28.8 %reduce-scatter.39.cloned.1.call-done = f32[64,4096]{1,0:T(8,128)} async-done(((f32[128,4096]{1,0:T(8,128)}), f32[64,4096]{1,0:T(8,128)}) %reduce-scatter.39.cloned.1.call-update) | async-done | bytes 1048592
  995.5 16.1 %reduce-scatter.25.cloned.1.call-done = f32[256,1024]{1,0:T(8,128)} async-done(((f32[512,1024]{1,0:T(8,128)}), f32[256,1024]{1,0:T(8,128)}) %reduce-scatter.25.cloned.1.call-update) | async-done | bytes 1048592 | tf_op jit(solution)/shard_map/reduce_scatter | solution.py:26
  1014.9 29.4 %reduce-scatter.37.cloned.1.call-done = f32[64,4096]{1,0:T(8,128)} async-done(((f32[128,4096]{1,0:T(8,128)}), f32[64,4096]{1,0:T(8,128)}) %reduce-scatter.37.cloned.1.call-update) | async-done | bytes 1048592
  1054.2 10.8 all-gather.31.cloned.1.call-done
  1065.1 21.1 %all-gather.25.cloned.1.call-done = bf16[128,4096]{1,0:T(8,128)(2,1)} async-done(((bf16[64,4096]{1,0:T(8,128)(2,1)}), bf16[128,4096]{1,0:T(8,128)(2,1)}) %all-gather.25.cloned.1.call-update) | async-done | bytes 1048592 | tf_op jit(solution)/shard_map/all_gather | solution.py:31
  1086.2 21.1 %all-gather.19.cloned.1.call-done = bf16[512,1024]{1,0:T(8,128)(2,1)} async-done(((bf16[256,1024]{1,0:T(8,128)(2,1)}), bf16[512,1024]{1,0:T(8,128)(2,1)}) %all-gather.19.cloned.1.call-update) | async-done | bytes 1048592 | tf_op jit(solution)/shard_map/all_gather | solution.py:31
  1107.4 21.1 %all-gather.13.cloned.1.call-done = bf16[128,4096]{1,0:T(8,128)(2,1)} async-done(((bf16[64,4096]{1,0:T(8,128)(2,1)}), bf16[128,4096]{1,0:T(8,128)(2,1)}) %all-gather.13.cloned.1.call-update) | async-done | bytes 1048592 | tf_op jit(solution)/shard_map/all_gather | solution.py:31
  1128.5 32.4 %all-gather.33.cloned.1.call-done = bf16[1024,1024]{1,0:T(8,128)(2,1)} async-done(((bf16[512,1024]{1,0:T(8,128)(2,1)}), bf16[1024,1024]{1,0:T(8,128)(2,1)}) %all-gather.33.cloned.1.call-update) | async-done | bytes 2097168 | tf_op jit(solution)/shard_map/all_gather | solution.py:31
  1161.0 32.4 %all-gather.27.cloned.1.call-done = bf16[256,4096]{1,0:T(8,128)(2,1)} async-done(((bf16[128,4096]{1,0:T(8,128)(2,1)}), bf16[256,4096]{1,0:T(8,128)(2,1)}) %all-gather.27.cloned.1.call-update) | async-done | bytes 2097168 | tf_op jit(solution)/shard_map/all_gather | solution.py:31
  1193.4 32.5 %all-gather.21.cloned.1.call-done = bf16[1024,1024]{1,0:T(8,128)(2,1)} async-done(((bf16[512,1024]{1,0:T(8,128)(2,1)}), bf16[1024,1024]{1,0:T(8,128)(2,1)}) %all-gather.21.cloned.1.call-update) | async-done | bytes 2097168 | tf_op jit(solution)/shard_map/all_gather | solution.py:31
  1226.0 32.4 %all-gather.15.cloned.1.call-done = bf16[256,4096]{1,0:T(8,128)(2,1)} async-done(((bf16[128,4096]{1,0:T(8,128)(2,1)}), bf16[256,4096]{1,0:T(8,128)(2,1)}) %all-gather.15.cloned.1.call-update) | async-done | bytes 2097168 | tf_op jit(solution)/shard_map/all_gather | solution.py:31
  1258.4 42.9 %add_convert_fusion = bf16[4096,1024]{1,0:T(8,128)(2,1)} fusion(bf16[4096,1024]{1,0:T(8,128)(2,1)} %add_convert_fusion.1, bf16[4096,4096]{1,0:T(8,128)(2,1)} %fusion.7, bf16[1024,4096]{1,0:T(8,128)(2,1)} %param.12), kind=kOutput, calls=%fused_computation.37 | convolution fusion | flops 34372321280 | bytes 58720256 | tf_op jit(solution)/shard_map/dot_general | solution.py:56
  1316.6 58.2 %all-gather.29.cloned.1.call-done = bf16[1024,4096]{1,0:T(8,128)(2,1)} async-done(((bf16[256,4096]{1,0:T(8,128)(2,1)}), bf16[1024,4096]{1,0:T(8,128)(2,1)}) %all-gather.29.cloned.1.call-update) | async-done | bytes 8388624 | tf_op jit(solution)/shard_map/all_gather | solution.py:31
  1374.8 58.2 %all-gather.23.cloned.1.call-done = bf16[4096,1024]{1,0:T(8,128)(2,1)} async-done(((bf16[1024,1024]{1,0:T(8,128)(2,1)}), bf16[4096,1024]{1,0:T(8,128)(2,1)}) %all-gather.23.cloned.1.call-update) | async-done | bytes 8388624 | tf_op jit(solution)/shard_map/all_gather | solution.py:31
  1433.0 58.1 %all-gather.17.cloned.1.call-done = bf16[1024,4096]{1,0:T(8,128)(2,1)} async-done(((bf16[256,4096]{1,0:T(8,128)(2,1)}), bf16[1024,4096]{1,0:T(8,128)(2,1)}) %all-gather.17.cloned.1.call-update) | async-done | bytes 8388624 | tf_op jit(solution)/shard_map/all_gather | solution.py:31
  (78 shorter events, 87.5 us)
Async XLA Ops:
  7.2 545.7 %reduce-scatter.31.cloned.1.call-start = ((), (), s32[]{:S(2)}) async-start(), calls=%async_computation.28 | async-start | bytes 20971520 | tf_op jit(solution)/shard_map/reduce_scatter | solution.py:26
  199.0 354.5 %reduce-scatter.27.cloned.1.call-start = ((), (), s32[]{:S(2)}) async-start(), calls=%async_computation.23 | async-start | bytes 20971520 | tf_op jit(solution)/shard_map/reduce_scatter | solution.py:26
  199.1 85.2 %copy-start.2 = (bf16[4096,1024]{1,0:T(8,128)(2,1)S(1)}, bf16[4096,1024]{1,0:T(8,128)(2,1)}, u32[]{:S(2)}) copy-start(bf16[4096,1024]{1,0:T(8,128)(2,1)} %add_convert_fusion.2) | copy-start | bytes 25165828
  326.9 246.7 %reduce-scatter.21.cloned.1.call-start = ((), (), s32[]{:S(2)}) async-start(), calls=%async_computation.17 | async-start | bytes 20971520 | tf_op jit(solution)/shard_map/reduce_scatter | solution.py:26
  425.4 271.3 %reduce-scatter.17.cloned.1.call-start = ((), (), s32[]{:S(2)}) async-start(), calls=%async_computation.12 | async-start | bytes 20971520 | tf_op jit(solution)/shard_map/reduce_scatter | solution.py:26
  425.5 85.2 %copy-start.1 = (bf16[4096,1024]{1,0:T(8,128)(2,1)S(1)}, bf16[4096,1024]{1,0:T(8,128)(2,1)}, u32[]{:S(2)}) copy-start(bf16[4096,1024]{1,0:T(8,128)(2,1)} %param.10) | copy-start | bytes 25165828
  552.8 367.0 %copy-start = (f32[64,4096]{1,0:T(8,128)S(1)}, f32[64,4096]{1,0:T(8,128)}, u32[]{:S(2)}) copy-start(f32[64,4096]{1,0:T(8,128)} %param.18) | copy-start | bytes 3145732
  552.8 198.4 %reduce-scatter.33.cloned.1.call-start = ((), (), s32[]{:S(2)}) async-start(), calls=%async_computation.29 | async-start | bytes 6291456 | tf_op jit(solution)/shard_map/reduce_scatter | solution.py:26
  553.4 252.4 %reduce-scatter.29.cloned.1.call-start = ((), (), s32[]{:S(2)}) async-start(), calls=%async_computation.24 | async-start | bytes 6291456 | tf_op jit(solution)/shard_map/reduce_scatter | solution.py:26
  554.0 306.5 %reduce-scatter.23.cloned.1.call-start = ((), (), s32[]{:S(2)}) async-start(), calls=%async_computation.18 | async-start | bytes 6291456 | tf_op jit(solution)/shard_map/reduce_scatter | solution.py:26
  573.7 341.6 %reduce-scatter.19.cloned.1.call-start = ((), (), s32[]{:S(2)}) async-start(), calls=%async_computation.13 | async-start | bytes 6291456 | tf_op jit(solution)/shard_map/reduce_scatter | solution.py:26
  696.7 250.7 %reduce-scatter.35.cloned.1.call-start = ((), (), s32[]{:S(2)}) async-start(), calls=%async_computation.30 | async-start | bytes 3145728 | tf_op jit(solution)/shard_map/reduce_scatter | solution.py:26
  751.3 228.2 %reduce-scatter.39.cloned.1.call-start = ((), (), s32[]{:S(2)}) async-start(), calls=%async_computation.35 | async-start | bytes 3145728
  805.8 205.8 %reduce-scatter.25.cloned.1.call-start = ((), (), s32[]{:S(2)}) async-start(), calls=%async_computation.19 | async-start | bytes 3145728 | tf_op jit(solution)/shard_map/reduce_scatter | solution.py:26
  860.5 183.8 %reduce-scatter.37.cloned.1.call-start = ((), (), s32[]{:S(2)}) async-start(), calls=%async_computation.34 | async-start | bytes 3145728
  918.1 146.9 %all-gather.31.cloned.1.call-start = ((), (), s32[]{:S(2)}) async-start(), calls=%async_computation.31 | async-start | bytes 1572864 | tf_op jit(solution)/shard_map/all_gather | solution.py:31
  950.6 135.5 %all-gather.25.cloned.1.call-start = ((), (), s32[]{:S(2)}) async-start(), calls=%async_computation.25 | async-start | bytes 1572864 | tf_op jit(solution)/shard_map/all_gather | solution.py:31
  988.7 118.6 %all-gather.19.cloned.1.call-start = ((), (), s32[]{:S(2)}) async-start(), calls=%async_computation.20 | async-start | bytes 1572864 | tf_op jit(solution)/shard_map/all_gather | solution.py:31
  1014.9 113.6 %all-gather.13.cloned.1.call-start = ((), (), s32[]{:S(2)}) async-start(), calls=%async_computation.14 | async-start | bytes 1572864 | tf_op jit(solution)/shard_map/all_gather | solution.py:31
  1054.2 106.7 %all-gather.33.cloned.1.call-start = ((), (), s32[]{:S(2)}) async-start(), calls=%async_computation.32 | async-start | bytes 3145728 | tf_op jit(solution)/shard_map/all_gather | solution.py:31
  1065.0 128.3 %all-gather.27.cloned.1.call-start = ((), (), s32[]{:S(2)}) async-start(), calls=%async_computation.26 | async-start | bytes 3145728 | tf_op jit(solution)/shard_map/all_gather | solution.py:31
  1086.2 139.8 %all-gather.21.cloned.1.call-start = ((), (), s32[]{:S(2)}) async-start(), calls=%async_computation.21 | async-start | bytes 3145728 | tf_op jit(solution)/shard_map/all_gather | solution.py:31
  1107.3 151.1 %all-gather.15.cloned.1.call-start = ((), (), s32[]{:S(2)}) async-start(), calls=%async_computation.15 | async-start | bytes 3145728 | tf_op jit(solution)/shard_map/all_gather | solution.py:31
  1128.5 188.1 %all-gather.35.cloned.1.call-start = ((), (), s32[]{:S(2)}) async-start(), calls=%async_computation.33 | async-start | bytes 10485760 | tf_op jit(solution)/shard_map/all_gather | solution.py:31
  1160.9 213.9 %all-gather.29.cloned.1.call-start = ((), (), s32[]{:S(2)}) async-start(), calls=%async_computation.27 | async-start | bytes 10485760 | tf_op jit(solution)/shard_map/all_gather | solution.py:31
  1193.4 239.6 %all-gather.23.cloned.1.call-start = ((), (), s32[]{:S(2)}) async-start(), calls=%async_computation.22 | async-start | bytes 10485760 | tf_op jit(solution)/shard_map/all_gather | solution.py:31
  1226.0 265.1 %all-gather.17.cloned.1.call-start = ((), (), s32[]{:S(2)}) async-start(), calls=%async_computation.16 | async-start | bytes 10485760 | tf_op jit(solution)/shard_map/all_gather | solution.py:31
Sparse Core Ops, SparseCore 0:
  199.1 123.3 reduce-scatter.30
  327.1 123.3 reduce-scatter.26
  453.0 120.5 reduce-scatter.20
  576.1 120.5 reduce-scatter.16
  698.8 52.4 reduce-scatter.32
  753.4 52.4 reduce-scatter.28
  808.1 52.3 reduce-scatter.22
  862.8 52.4 reduce-scatter.18
  917.5 29.9 reduce-scatter.34
  949.5 29.9 reduce-scatter.38
  981.7 29.9 reduce-scatter.24
  1014.3 29.9 reduce-scatter.36
  1045.8 19.1 all-gather.30
  1067.0 19.1 all-gather.24
  1088.1 19.1 all-gather.18
  1109.3 19.1 all-gather.12
  1129.8 31.0 all-gather.32
  1162.3 31.0 all-gather.26
  1194.9 31.0 all-gather.20
  1227.3 31.0 all-gather.14
  1260.0 56.6 all-gather.34
  1318.2 56.6 all-gather.28
  1376.4 56.6 all-gather.22
  1434.4 56.6 all-gather.16
where the time goes:
time: 1540 us; the launch traced here: 1530 us
  waiting for transfers between devices  851 us (55%)
  matrix products  588 us (38%)
  local copies, waits for them, and re-layouts  59.9 us (4%)
    reduce_scatter x10, waiting for transfers between devices, reduce_scatter(): s = lax.psum_scatter(s, ax, scatter_dimension=0, tiled=True)  403 us
    all_gather x12, waiting for transfers between devices, all_gather(): w = lax.all_gather(w, ax, axis=0, tiled=True)  389 us
    dot_general x1, matrix products, local(): dh1 = jnp.dot(dh2, w2.T, preferred_element_type=f32).astype(bf)  85.2 us
    dot_general x1, matrix products, local(): dh3 = jnp.dot(g, w4.T, preferred_element_type=f32).astype(bf)  85.2 us
    unnamed x26, waiting for transfers between devices  59.5 us
    dot_general x1, matrix products, local(): s4 = reduce_scatter(jnp.dot(h3.T, g, preferred_element_type=f32))  55.5 us
    dot_general x1, matrix products, local(): s2 = reduce_scatter(jnp.dot(h1.T, dh2, preferred_element_type=f32))  55.5 us
    unnamed x19, local copies, waits for them, and re-layouts  52.3 us
  transfers between devices with their start and end apart: 24, of which 22 were waited for; matrix products, arithmetic and copies ran while one was open for 29% of the time, Pallas kernels for 0%

commit v1 on v0

v1 whole, which is shorter than its diff:
```python
import jax
import jax.numpy as jnp
from jax import lax
from jax.experimental import pallas as pl
from jax.experimental.pallas import tpu as pltpu
from jax.sharding import PartitionSpec as P

LR = 0.0005
MU = 0.9
DATA = ("dx", "dy", "dz")
C0 = 0.7978845608028654
C1 = 0.044715
T, D, F = 4096, 1024, 4096
BIG, HALF, QUART, GRP, BLK, CH = 1024, 512, 256, 128, 64, 16
f32, bf = jnp.float32, jnp.bfloat16
MESH = pl.DeviceIdType.MESH
VLIM = 63 * 2**20
NN = (((1,), (0,)), ((), ()))
NT = (((1,), (1,)), ((), ()))
TN = (((0,), (0,)), ((), ()))
CORE, SA, SB, SC, GY, GX, GZ, GC, GD = range(9)
DEPTH = {CORE: 3, SA: 3, SB: 3, SC: 3}
UNITS = 16
PART = 8
OFF_A = ((5, 8, 16, 21, 31, 34, 42, 51, 58), (4, 6, 13, 19, 28, 31, 38, 48, 60))
OFF_B = ((7, 8, 16, 21, 27, 32, 37, 44, 54), (7, 8, 14, 19, 23, 30, 33, 41, 51))


def _dot(a, b, dims):
    return lax.dot_general(a, b, dims, preferred_element_type=f32)


def _gelu_both(z):
    s = z * z
    t = jnp.tanh(z * (C0 + (C0 * C1) * s))
    w = 0.5 + 0.5 * t
    return z * w, w + (w * (1.0 - t)) * (z * (C0 + (3.0 * C0 * C1) * s))


def _gelu(z):
    return _gelu_both(z)[0]


def _gelu_grad(z):
    return _gelu_both(z)[1]


def _loop(n, body):
    def step(k, _):
        body(k)
        return 0
    lax.fori_loop(0, n, step, 0)


def _ds(start, size):
    return pl.ds(pl.multiple_of(start, size), size)


def _cut(k, size):
    return slice(k * size, (k + 1) * size)


def _fwd_kernel(x_ref, w1_ref, w2_ref, z1_ref, h1_ref, h2_ref):
    x = x_ref[...]
    for j in range(F // HALF):
        sl = _cut(j, HALF)
        z = jnp.dot(x, w1_ref[:, sl], preferred_element_type=f32).astype(bf)
        z1_ref[:, sl] = z
        h1_ref[:, sl] = _gelu(z.astype(f32)).astype(bf)
    h2 = jnp.dot(h1_ref[...], w2_ref[...], preferred_element_type=f32) + x.astype(f32)
    h2_ref[...] = h2.astype(bf)


def _row(m, n):
    return pl.BlockSpec((m, n), lambda i: (i, 0))


def _fwd(x, w1, w2):
    res = lambda s: pl.BlockSpec(s, lambda i: (0, 0), pipeline_mode=pl.Buffered(1))
    sh = lambda n: jax.ShapeDtypeStruct((T, n), bf)
    return pl.pallas_call(
        _fwd_kernel, grid=(T // HALF,),
        in_specs=[_row(HALF, D), res((D, F)), res((F, D))],
        out_specs=[_row(HALF, F), _row(HALF, F), _row(HALF, D)],
        out_shape=[sh(F), sh(F), sh(D)],
        compiler_params=pltpu.CompilerParams(vmem_limit_bytes=VLIM, dimension_semantics=("arbitrary",)),
        name="fwd")(x, w1, w2)


def _xor(a, b):
    return a + b - 2 * a * b


def _pick(s, a, b):
    return a + s * (b - a)


def _tile(t):
    return t % 2, (t // 2) % 2, t // 4


def _owner(t, i, j):
    g, be, ga = _tile(t)
    b, c = _xor(_xor(i, j), be), _xor(j, ga)
    return _pick(g, j, c), _pick(g, b, j), _pick(g, c, b)


def _block(x, c, y, z):
    return x * 8 + c * 4 + y * 2 + z


def _mid_kernel(x_h, g_h, w1_h, w2_h, w3_h, w4_h, m1_h, m2_h, m3_h, m4_h, z1_h, h1_h, h2_h,
                dz3_h, dz1_h, dx_h, wa_h, wb_h, ma_h, mb_h,
                R0, R1, TT, WA, WB, UA, UB, RcA, RcB, RaA, RaB, RbA, RbB, RdA, RdB,
                mA, wA, oA, mB, wB, oB, init_sem, w_sem, t_sem, o_sem, m_sem, ssem, rsem, gssem, grsem, cred):
    dx, my, mz = lax.axis_index("dx"), lax.axis_index("dy"), lax.axis_index("dz")
    mc, mx = dx % 2, dx // 2
    me = _block(mx, mc, my, mz)

    def dev(cc=0, x=0, y=0, z=0):
        return {"dx": _xor(mx, x) * 2 + _xor(mc, cc), "dy": _xor(my, y), "dz": _xor(mz, z)}

    core, devx, devy, devz = dev(cc=1), dev(x=1), dev(y=1), dev(z=1)
    ACROSS = {CORE: lambda col: core, SA: lambda col: dev(x=1 - col, y=col), SB: lambda col: dev(y=1 - col, z=col),
              SC: lambda col: dev(z=1 - col, x=col)}

    barrier = pltpu.get_barrier_semaphore()
    for d in (core, devx, devy, devz):
        pl.semaphore_signal(barrier, inc=1, device_id=d, device_id_type=MESH)
    pl.semaphore_wait(barrier, 4)

    def copies(pairs, sem):
        for a, b in pairs:
            pltpu.make_async_copy(a, b, sem).start()

    def landed(ref, sem):
        pltpu.make_async_copy(ref, ref, sem).wait()

    def cols(t):
        out = []
        for q in range(4):
            x, y, z = _owner(t, q // 2, q % 2)
            out.append(pl.multiple_of(_block(x, q // 2, y, z) * QUART + (t % 2) * GRP, GRP))
        return list(enumerate(out))

    def load_wa(t, w):
        s = t % 2
        copies([(w.at[:, pl.ds(c, GRP)], WA.at[s, :, _ds(GRP * q, GRP)]) for q, c in cols(t)], w_sem.at[0, s])

    def load_wb(t, w):
        s = t % 2
        copies([(w.at[pl.ds(c, GRP), :], WB.at[s, _ds(GRP * q, GRP), :]) for q, c in cols(t)], w_sem.at[1, s])

    def load_cols(t, a, k):
        copies([(a.at[:, pl.ds(c, GRP)], TT.at[k, :, _ds(GRP * q, GRP)]) for q, c in cols(t)], t_sem.at[k])

    def tile_in(k):
        landed(TT.at[k], t_sem.at[k])

    def store_cols(t, a):
        copies([(TT.at[1, :, _ds(GRP * q, GRP)], a.at[:, pl.ds(c, GRP)]) for q, c in cols(t)], o_sem.at[0])

    def stored():
        landed(TT.at[1], o_sem.at[0])

    def rc(ty, st, n, src, dst, d):
        s = n % DEPTH[st]
        return pltpu.make_async_remote_copy(src_ref=src, dst_ref=dst, send_sem=ssem.at[ty, st, s],
                                            recv_sem=rsem.at[ty, st, s], device_id=d, device_id_type=MESH)

    def gc(ty, st, n, ref, d):
        return pltpu.make_async_remote_copy(src_ref=ref, dst_ref=ref, send_sem=gssem.at[ty, st - GY, n],
                                            recv_sem=grsem.at[ty, st - GY, n], device_id=d, device_id_type=MESH)

    def take(ty, st, n):
        @pl.when(n >= DEPTH[st])
        def _():
            pl.semaphore_wait(cred.at[ty, st, n % DEPTH[st]], 1)

    def give(ty, st, n):
        m = n + DEPTH[st]

        @pl.when(m < UNITS)
        def _():
            pl.semaphore_signal(cred.at[ty, st, n % DEPTH[st]], inc=1, device_id=ACROSS[st](_xor(m % 2, ty)),
                                device_id_type=MESH)

    def add_rows(dst, src):
        def body(k):
            r = _ds(k * 2 * CH, 2 * CH)
            dst[r, :] = dst[r, :] + src[r, :]
        _loop(GRP // (2 * CH), body)

    def add_blocks(dst, src, count):
        def body(k):
            dst[k] = dst[k] + src[k]
        _loop(count, body)

    def update(m_ref, w_ref, o_ref, a_ref, b_ref, rows):
        def body(k):
            r = _ds(k * CH, CH)
            m = MU * m_ref[r, :] + (a_ref[r, :] + b_ref[r, :]) * (1.0 / UNITS)
            m_ref[r, :] = m
            o_ref[r, :] = (w_ref[r, :].astype(f32) - LR * m).astype(bf)
        _loop(rows // CH, body)

    def by_half(n, lo, hi):
        pl.when(n < PART)(lo)
        pl.when(n >= PART)(hi)

    def a_piece(n, i, z):
        g, be, ga = _tile(n % PART)
        j = _pick(g, _xor(z, ga), _xor(_xor(z, i), be))
        x, y, _ = _owner(n % PART, i, j)
        rows = pl.ds(pl.multiple_of(_block(x, i, y, z) * QUART + g * GRP, GRP), GRP)
        return wa_h.at[n // PART, rows, :], x, y

    def a_info(n):
        g, be, ga = _tile(n % PART)
        x, y, z = _owner(n % PART, mc, _pick(g, mx, my))
        snd = _pick(g, _xor(y, my), _xor(z, mz)) == 1
        last = _pick(g, _xor(z, mz), _xor(x, mx)) == 0
        keep = jnp.logical_not(snd)
        return snd, keep, keep & jnp.logical_not(last), keep & last

    def a_core(n):
        return rc(0, CORE, n, UA.at[pl.ds(2, 2)], RcA.at[n % DEPTH[CORE]], core)

    def a_sa(n):
        return rc(0, SA, n, RcA.at[n % DEPTH[CORE], 1], RaA.at[n % DEPTH[SA]], ACROSS[SA](n % 2))

    def a_sb(n):
        return rc(0, SB, n, RaA.at[n % DEPTH[SA]], RbA.at[n % DEPTH[SB]], ACROSS[SB](n % 2))

    def a_sc(n):
        return rc(0, SC, n, RbA.at[n % DEPTH[SB]], RdA.at[n % DEPTH[SC]], ACROSS[SC](n % 2))

    def a0(n):
        take(0, CORE, n)
        a_core(n).start()

    def a1(n):
        a_core(n).wait()
        for k in range(2):
            add_rows(RcA.at[n % DEPTH[CORE], k], UA.at[k])
        take(0, SA, n)
        a_sa(n).start()

    def a2(n):
        snd, keep, pas, fin = a_info(n)
        a_sa(n).wait()
        add_rows(RaA.at[n % DEPTH[SA]], RcA.at[n % DEPTH[CORE], 0])
        give(0, CORE, n)
        take(0, SB, n)
        pl.when(snd)(lambda: a_sb(n).start())

    def a3(n):
        snd, keep, pas, fin = a_info(n)
        pl.when(snd)(lambda: a_sb(n).wait_send())

        @pl.when(keep)
        def _():
            a_sb(n).wait_recv()
            add_rows(RbA.at[n % DEPTH[SB]], RaA.at[n % DEPTH[SA]])
        give(0, SA, n)
        take(0, SC, n)
        pl.when(pas)(lambda: a_sc(n).start())

        @pl.when(fin)
        def _():
            s = n % 2

            def load(m, w):
                pltpu.make_async_copy(m.at[_ds(s * GRP, GRP), :], mA.at[s], m_sem.at[0, 0, s]).start()
                pltpu.make_async_copy(w.at[pl.ds(pl.multiple_of(me * QUART + s * GRP, GRP), GRP), :], wA.at[s],
                                      m_sem.at[0, 1, s]).start()
            by_half(n, lambda: load(m4_h, w4_h), lambda: load(m2_h, w2_h))

    def a4(n):
        snd, keep, pas, fin = a_info(n)
        pl.when(pas)(lambda: a_sc(n).wait_send())

        @pl.when(fin)
        def _():
            s = n % 2
            a_sc(n).wait_recv()
            landed(mA.at[s], m_sem.at[0, 0, s])
            landed(wA.at[s], m_sem.at[0, 1, s])
            update(mA.at[s], wA.at[s], oA.at[s], RbA.at[n % DEPTH[SB]], RdA.at[n % DEPTH[SC]], GRP)
            out, _, _ = a_piece(n, mc, mz)
            pltpu.make_async_copy(mA.at[s], ma_h.at[n // PART, _ds(s * GRP, GRP), :], m_sem.at[0, 2, s]).start()
            pltpu.make_async_copy(oA.at[s], out, m_sem.at[0, 3, s]).start()
            pltpu.make_async_remote_copy(src_ref=oA.at[s], dst_ref=out, send_sem=gssem.at[0, 0, n],
                                         recv_sem=grsem.at[0, 0, n], device_id=devy, device_id_type=MESH).start()
        give(0, SB, n)
        give(0, SC, n)

    def a5(n):
        ref, x, y = a_piece(n, mc, mz)
        isx, isy = mx == x, my == y

        @pl.when(isx & isy)
        def _():
            s = n % 2
            gc(0, GY, n, ref, devy).wait_send()
            landed(mA.at[s], m_sem.at[0, 2, s])
            landed(oA.at[s], m_sem.at[0, 3, s])
        pl.when(isx & jnp.logical_not(isy))(lambda: gc(0, GY, n, ref, devy).wait_recv())
        pl.when(isx)(lambda: gc(0, GX, n, ref, devx).start())

    def a6(n):
        ref, x, y = a_piece(n, mc, mz)
        pl.when(mx == x)(lambda: gc(0, GX, n, ref, devx).wait_send())
        pl.when(mx != x)(lambda: gc(0, GX, n, ref, devx).wait_recv())
        gc(0, GZ, n, ref, devz).start()

    def a7(n):
        ref, _, _ = a_piece(n, mc, mz)
        gc(0, GZ, n, ref, devz).wait()
        gc(0, GC, n, ref, core).start()
        gc(0, GD, n, a_piece(n, mc, 1 - mz)[0], core).start()

    def a8(n):
        ref, _, _ = a_piece(n, mc, mz)
        gc(0, GC, n, ref, core).wait()
        gc(0, GD, n, ref, core).wait()

    def b_core(n):
        return rc(1, CORE, n, UB.at[pl.ds(8, 8)], RcB.at[n % DEPTH[CORE]], core)

    def b_sa(n):
        return rc(1, SA, n, RcB.at[n % DEPTH[CORE], pl.ds(4, 4)], RaB.at[n % DEPTH[SA]], ACROSS[SA](1 - n % 2))

    def b_sb(n):
        return rc(1, SB, n, RaB.at[n % DEPTH[SA], pl.ds(2, 2)], RbB.at[n % DEPTH[SB]], ACROSS[SB](1 - n % 2))

    def b_sc(n):
        return rc(1, SC, n, RbB.at[n % DEPTH[SB], 1], RdB.at[n % DEPTH[SC]], ACROSS[SC](1 - n % 2))

    def b_out(n, count):
        q = mc * 8 + mz * 4 + mx * 2 + my
        return wb_h.at[n // PART, n % PART, pl.ds(q // count * count, count)]

    def b0(n):
        take(1, CORE, n)
        b_core(n).start()

    def b1(n):
        b_core(n).wait()
        add_blocks(RcB.at[n % DEPTH[CORE]], UB, 8)
        take(1, SA, n)
        b_sa(n).start()

    def b2(n):
        b_sa(n).wait()
        add_blocks(RaB.at[n % DEPTH[SA]], RcB.at[n % DEPTH[CORE]], 4)
        give(1, CORE, n)
        take(1, SB, n)
        b_sb(n).start()

    def b3(n):
        b_sb(n).wait()
        add_blocks(RbB.at[n % DEPTH[SB]], RaB.at[n % DEPTH[SA]], 2)
        give(1, SA, n)
        take(1, SC, n)
        b_sc(n).start()
        s = n % 2

        def load(m, w):
            copies([(m.at[:, pl.ds(c, GRP)], mB.at[s, :, _ds(GRP * q, GRP)]) for q, c in cols(n % PART)],
                   m_sem.at[1, 0, s])
            copies([(w.at[_ds(me * BLK, BLK), pl.ds(c, GRP)], wB.at[s, :, _ds(GRP * q, GRP)])
                    for q, c in cols(n % PART)], m_sem.at[1, 1, s])
        by_half(n, lambda: load(m3_h, w3_h), lambda: load(m1_h, w1_h))

    def b4(n):
        s = n % 2
        b_sc(n).wait()
        landed(mB.at[s], m_sem.at[1, 0, s])
        landed(wB.at[s], m_sem.at[1, 1, s])
        update(mB.at[s], wB.at[s], oB.at[s, 0], RbB.at[n % DEPTH[SB], 0], RdB.at[n % DEPTH[SC]], BLK)
        copies([(mB.at[s, :, _ds(GRP * q, GRP)], mb_h.at[n // PART, :, pl.ds(c, GRP)]) for q, c in cols(n % PART)],
               m_sem.at[1, 2, s])
        pltpu.make_async_copy(oB.at[s], b_out(n, 1), m_sem.at[1, 3, s]).start()
        give(1, SB, n)
        give(1, SC, n)
        pltpu.make_async_remote_copy(src_ref=oB.at[s], dst_ref=b_out(n, 1), send_sem=gssem.at[1, 0, n],
                                     recv_sem=grsem.at[1, 0, n], device_id=devy, device_id_type=MESH).start()

    def b5(n):
        s = n % 2
        gc(1, GY, n, b_out(n, 1), devy).wait()
        landed(mB.at[s], m_sem.at[1, 2, s])
        landed(oB.at[s], m_sem.at[1, 3, s])
        gc(1, GX, n, b_out(n, 2), devx).start()

    def b6(n):
        gc(1, GX, n, b_out(n, 2), devx).wait()
        gc(1, GZ, n, b_out(n, 4), devz).start()

    def b7(n):
        gc(1, GZ, n, b_out(n, 4), devz).wait()
        gc(1, GC, n, b_out(n, 8), core).start()

    def b8(n):
        gc(1, GC, n, b_out(n, 8), core).wait()

    OPS = list(zip((a0, a1, a2, a3, a4, a5, a6, a7, a8), *OFF_A)) + list(zip((b0, b1, b2, b3, b4, b5, b6, b7, b8), *OFF_B))
    SPAN = max(max(o[1:]) for o in OPS)

    def exchange(v, k, lo, hi, v0, v1):
        for fn, first, second in sorted(OPS, key=lambda o: -o[1]):
            hits = []
            for off, s0, shift in ((first, 0, 0), (second, 10, 2)):
                lag, at = off // PART, off % PART
                if lo <= at < hi and v0 < s0 + PART + lag and v1 > s0 + lag:
                    hits.append(((v >= s0 + lag) & (v < s0 + PART + lag) & (k == at), v - lag - shift))
            if not hits:
                continue
            ok, n = hits[0]
            if len(hits) > 1:
                ok, n = ok | hits[1][0], jnp.where(ok, n, hits[1][1])
            pl.when(ok)(lambda fn=fn, n=n: fn(n))

    def s_rows(lhs, rhs, j, n):
        a = _pick(n % 2, mx, my)
        r = _dot(lhs[:, _ds(j * QUART, QUART)], rhs[...], TN)
        p = _xor(j, mc) * 2
        UA[p + a] = r[:GRP]
        UA[p + (1 - a)] = r[GRP:]

    def s_cols(lhs, rhs, j, n):
        col = 1 - n % 2
        r = _dot(lhs[:, _ds(j * HALF, HALF)], rhs[...], TN)
        px = _xor(j, mx)
        for k in range(PART):
            pc, py, pz = _xor(k // 4, mc), _xor((k // 2) % 2, my), _xor(k % 2, mz)
            UB[_block(pc, _pick(col, px, py), _pick(col, py, pz), _pick(col, pz, px))] = r[_cut(k, BLK)]

    def load_w_tiles(w, k0, dst):
        copies([(w.at[:, _ds(HALF * (k0 + k), HALF)], TT.at[dst, _ds(BIG * k, BIG), :]) for k in range(4)], t_sem.at[dst])

    def load_row_tile(a, i):
        d = 2 - i % 2
        copies([(a.at[_ds(HALF * i, HALF), _ds(HALF * k, HALF)], TT.at[d, _ds(HALF * k, HALF), :]) for k in range(PART)],
               t_sem.at[d])

    def row_tile(kk, a, add, out, then):
        i, hh = kk // 2, kk % 2
        d = 2 - i % 2

        @pl.when(hh == 0)
        def _():
            tile_in(d)
            pl.when(i < PART - 1)(lambda: load_row_tile(a, i + 1))
            pl.when(i == PART - 1)(then)
        rows, half = _ds(i * HALF, HALF), _ds(hh * HALF, HALF)
        acc = None
        for k in range(PART):
            w = TT[3 * (k // 4), _ds(BIG * (k % 4) + hh * HALF, HALF), :]
            p = _dot(TT[d, _cut(k, HALF), :], w, NT)
            acc = p if acc is None else acc + p
        out[rows, half] = (acc + add[rows, half].astype(f32)).astype(bf)

    load_wa(0, w3_h)
    load_wb(0, w4_h)
    for k in range(4):
        rows = _ds(k * BIG, BIG)
        pltpu.make_async_copy(h2_h.at[rows, :], R0.at[rows, :], init_sem.at[0, k]).start()
        pltpu.make_async_copy(g_h.at[rows, :], R1.at[rows, :], init_sem.at[1, k]).start()

    def step12(v):
        s = v % 2
        landed(WA.at[s], w_sem.at[0, s])
        landed(WB.at[s], w_sem.at[1, s])
        pl.when(v >= 1)(stored)
        pl.when(v == PART - 1)(lambda: load_w_tiles(w3_h, 4, 3))

        def d1(j):
            rows = _ds(j * BIG, BIG)

            @pl.when(v == 0)
            def _():
                landed(R0.at[rows, :], init_sem.at[0, j])
                landed(R1.at[rows, :], init_sem.at[1, j])
            z = _dot(R0[rows, :], WA[s], NN).astype(bf)
            dh = _dot(R1[rows, :], WB[s], NT).astype(bf)
            h, d = _gelu_both(z.astype(f32))
            TT[0, rows, :] = h.astype(bf)
            TT[1, rows, :] = (d * dh.astype(f32)).astype(bf)
            exchange(v, j, 0, 4, 0, 8)
        _loop(4, d1)
        store_cols(v, dz3_h)

        @pl.when(v < PART - 1)
        def _():
            load_wa(v + 1, w3_h)
            load_wb(v + 1, w4_h)

        def d2(j):
            s_rows(TT.at[0], R1, j, v)
            exchange(v, j + 4, 4, 6, 0, 8)
        _loop(2, d2)

        @pl.when(v == PART - 1)
        def _():
            load_w_tiles(w3_h, 0, 0)
            load_wb(0, w2_h)
            stored()
            load_row_tile(dz3_h, 0)

        def d3(j):
            s_cols(R0, TT.at[1], j, v)
            exchange(v, j + 6, 6, 8, 0, 8)
        _loop(2, d3)
    _loop(PART, step12)

    tile_in(0)
    tile_in(3)

    def step3(kk):
        row_tile(kk, dz3_h, R1, R0, lambda: load_cols(0, h1_h, 2))
        exchange(8 + kk // PART, kk % PART, 0, 8, 8, 10)
    _loop(2 * PART, step3)
    pltpu.make_async_copy(x_h, R1, o_sem.at[1]).start()
    load_cols(0, z1_h, 0)

    def step4(t):
        s = t % 2
        v = t + 10
        n = t + PART
        landed(WB.at[s], w_sem.at[1, s])
        tile_in(2 + s)
        pl.when(t < PART - 1)(lambda: load_cols(t + 1, h1_h, 3 - s))

        def d4(j):
            s_rows(TT.at[2 + s], R0, j, n)
            exchange(v, j, 0, 2, 10, 18)
        _loop(2, d4)
        pl.when(t == PART - 1)(lambda: load_w_tiles(w1_h, 4, 3))
        tile_in(0)
        pl.when(t >= 1)(stored)

        def d5(j):
            for q in range(4):
                rows = _ds(j * BIG + q * QUART, QUART)
                dh = _dot(R0[rows, :], WB[s], NT).astype(bf)
                d = _gelu_grad(TT[0, rows, :].astype(f32))
                TT[1, rows, :] = (d * dh.astype(f32)).astype(bf)
            exchange(v, j + 2, 2, 6, 10, 18)
        _loop(4, d5)
        store_cols(t, dz1_h)

        @pl.when(t < PART - 1)
        def _():
            load_cols(t + 1, z1_h, 0)
            load_wb(t + 1, w2_h)
        pl.when(t == 0)(lambda: landed(R1, o_sem.at[1]))
        pl.when(t == PART - 1)(lambda: load_w_tiles(w1_h, 0, 0))

        def d6(j):
            s_cols(R1, TT.at[1], j, n)

            @pl.when((t == PART - 1) & (j == 0))
            def _():
                stored()
                load_row_tile(dz1_h, 0)
            exchange(v, j + 6, 6, 8, 10, 18)
        _loop(2, d6)
    _loop(PART, step4)

    tile_in(0)
    tile_in(3)

    def step5(kk):
        pl.when(kk < 2 * PART)(lambda: row_tile(kk, dz1_h, R0, R1, lambda: None))
        pl.when(kk == 2 * PART)(lambda: pltpu.make_async_copy(R1, dx_h, o_sem.at[2]).start())
        exchange(18 + kk // PART, kk % PART, 0, 8, 18, 18 + SPAN)
    _loop(SPAN, step5)
    landed(R1, o_sem.at[2])


def _mid(x, g, w1, w2, w3, w4, m1, m2, m3, m4, z1, h1, h2):
    anyspec = pl.BlockSpec(memory_space=pl.ANY)
    sd = jax.ShapeDtypeStruct
    V, DMA = pltpu.VMEM, pltpu.SemaphoreType.DMA
    dc, da, db, dd = (DEPTH[k] for k in (CORE, SA, SB, SC))
    return pl.pallas_call(
        _mid_kernel,
        in_specs=[anyspec] * 13,
        out_specs=[anyspec] * 7,
        out_shape=[sd((T, F), bf), sd((T, F), bf), sd((T, D), bf),
                   sd((2, F, D), bf), sd((2, PART, UNITS, BLK, HALF), bf), sd((2, QUART, D), f32), sd((2, BLK, F), f32)],
        scratch_shapes=[
            V((T, D), bf), V((T, D), bf), V((4, T, HALF), bf), V((2, D, HALF), bf), V((2, HALF, D), bf),
            V((4, GRP, D), f32), V((UNITS, BLK, HALF), f32),
            V((dc, 2, GRP, D), f32), V((dc, 8, BLK, HALF), f32),
            V((da, GRP, D), f32), V((da, 4, BLK, HALF), f32),
            V((db, GRP, D), f32), V((db, 2, BLK, HALF), f32),
            V((dd, GRP, D), f32), V((dd, BLK, HALF), f32),
            V((2, GRP, D), f32), V((2, GRP, D), bf), V((2, GRP, D), bf),
            V((2, BLK, HALF), f32), V((2, BLK, HALF), bf), V((2, 1, BLK, HALF), bf),
            DMA((2, 4)), DMA((2, 2)), DMA((4,)), DMA((3,)), DMA((2, 4, 2)),
            DMA((2, 4, dc)), DMA((2, 4, dc)), DMA((2, 5, UNITS)), DMA((2, 5, UNITS)),
            pltpu.SemaphoreType.REGULAR((2, 4, dc)),
        ],
        compiler_params=pltpu.CompilerParams(vmem_limit_bytes=VLIM, collective_id=0, has_side_effects=True),
        name="mid")(x, g, w1, w2, w3, w4, m1, m2, m3, m4, z1, h1, h2)


def _last_kernel(dx, wa1, wb1, wa0, wb0, ma1, mb1, ma0, mb0, dxn, w2n, w1n, w4n, w3n, m2n, m1n, m4n, m3n):
    dxn[...] = dx[...]
    for src, dst in ((wa1, w2n), (wa0, w4n), (ma1, m2n), (ma0, m4n), (mb1, m1n), (mb0, m3n)):
        dst[...] = src[0]
    for src, dst in ((wb1, w1n), (wb0, w3n)):
        for t in range(PART):
            for q in range(4):
                x, y, z = _owner(t, q // 2, q % 2)
                k = 2 * _block(x, q // 2, y, z) + t % 2
                dst[:, _cut(k, GRP)] = src[0, t, 0, :, _cut(q, GRP)]


def _last(dx, wa, wb, ma, mb):
    sd = jax.ShapeDtypeStruct
    col = lambda m, n: pl.BlockSpec((m, n), lambda i: (0, i))
    half = lambda h, m, n: pl.BlockSpec((1, m, n), lambda i: (h, i, 0))
    hcol = lambda h, m, n: pl.BlockSpec((1, m, n), lambda i: (h, 0, i))
    blk = lambda h: pl.BlockSpec((1, PART, 1, BLK, HALF), lambda i: (
        h, 0, (i // 4) % 2 * 8 + i % 2 * 4 + i // 8 * 2 + (i // 2) % 2, 0, 0))
    ins, outs, shapes = [_row(QUART, D)], [_row(QUART, D)], [sd((T, D), bf)]
    for h in (1, 0):
        ins += [half(h, QUART, D), blk(h)]
        outs += [_row(QUART, D), _row(BLK, F)]
        shapes += [sd((F, D), bf), sd((D, F), bf)]
    for h in (1, 0):
        ins += [half(h, CH, D), hcol(h, BLK, QUART)]
        outs += [_row(CH, D), col(BLK, QUART)]
        shapes += [sd((QUART, D), f32), sd((BLK, F), f32)]
    return pl.pallas_call(
        _last_kernel, grid=(UNITS,), in_specs=ins, out_specs=outs, out_shape=shapes,
        compiler_params=pltpu.CompilerParams(vmem_limit_bytes=VLIM, dimension_semantics=("arbitrary",)),
        name="last")(dx, wa, wb, wa, wb, ma, mb, ma, mb)


def solution(mesh):
    def local(x, g, w1, w2, w3, w4, m1, m2, m3, m4):
        z1, h1, h2 = _fwd(x, w1, w2)
        _, _, dx, wa, wb, ma, mb = _mid(x, g, w1, w2, w3, w4, m1, m2, m3, m4, z1, h1, h2)
        dx, w2n, w1n, w4n, w3n, m2n, m1n, m4n, m3n = _last(dx, wa, wb, ma, mb)
        return dx, w1n, w2n, w3n, w4n, m1n, m2n, m3n, m4n

    row, rep = P(DATA, None), P()
    return jax.shard_map(local, mesh=mesh,
                         in_specs=(row, row, rep, rep, rep, rep, row, row, row, row),
                         out_specs=(row, rep, rep, rep, rep, row, row, row, row),
                         check_vma=False)
```

time: 1540 us -> 587 us (0.38)
  waiting for transfers between devices: 851 us -> 0 us
  matrix products: 588 us -> 0 us
  Pallas kernels: 0 us -> 586 us
  local copies, waits for them, and re-layouts: 59.9 us -> 0 us
    dot_general x11 -> x0, matrix products: 588 us -> none  [the longest x1 85.2 us: local(): dh1 = jnp.dot(dh2, w2.T, preferred_element_type=f32).astype(bf)]
    pallas_call x0 -> x3, Pallas kernels: none -> 586 us  [the longest x1 462 us: _mid(): pl.pallas_call(_mid_kernel, in_specs=[anyspec] * 13, out_specs=[anyspec]...]
    reduce_scatter x10 -> x0, waiting for transfers between devices: 403 us -> none  [reduce_scatter(): s = lax.psum_scatter(s, ax, scatter_dimension=0, tiled=True)]
    all_gather x12 -> x0, waiting for transfers between devices: 389 us -> none  [all_gather(): w = lax.all_gather(w, ax, axis=0, tiled=True)]
    unnamed x26 -> x0, waiting for transfers between devices: 59.5 us -> none
    unnamed x19 -> x0, local copies, waits for them, and re-layouts: 52.3 us -> none
  transfers between devices with their start and end apart: 24 -> 0, of which waited for: 22 -> 0; matrix products, arithmetic and copies ran while one was open for 29% -> 0% of each run, Pallas kernels for 0% -> 0%
where the time goes in v1:
time: 587 us
  Pallas kernels  586 us (100%)
    pallas_call x1, Pallas kernels, _mid(): pl.pallas_call(_mid_kernel, in_specs=[anyspec] * 13, out_specs=[anyspec]...  462 us
    pallas_call x1, Pallas kernels, _fwd(): pl.pallas_call(_fwd_kernel, grid=(T // HALF,), in_specs=[_row(HALF, D), r...  90.1 us
    pallas_call x1, Pallas kernels, _last(): pl.pallas_call(_last_kernel, grid=(UNITS,), in_specs=ins, out_specs=outs,...  33.7 us

profile of v1, /device:TPU:0, one launch (start us, length us, event | category | flops | bytes accessed | tf_op | source)
XLA Modules:
  0.0 586.9 jit_solution(865911976182622726)
XLA Ops:
  0.6 90.1 %fwd.1 = (bf16[4096,4096]{1,0:T(8,128)(2,1)}, bf16[4096,4096]{1,0:T(8,128)(2,1)}, bf16[4096,1024]{1,0:T(8,128)(2,1)}) custom-call(bf16[4096,1024]{1,0:T(8,128)(2,1)} %x_h.1, bf16[1024,4096]{1,0:T(8,128)(2,1)} %w1_h.1, bf16[4096,1024]{1,0:T(8,128)(2,1)} %w2_h.1), custom_call_target="tpu_custom_call" | custom-call | tf_op jit(solution)/shard_map/fwd/pallas_call | solution.py:81
  90.8 462.2 %mid.1 = (bf16[4096,4096]{1,0:T(8,128)(2,1)}, bf16[4096,4096]{1,0:T(8,128)(2,1)}, bf16[4096,1024]{1,0:T(8,128)(2,1)}, bf16[2,4096,1024]{2,1,0:T(8,128)(2,1)}, bf...) custom-call(bf16[4096,1024]{1,0:T(8,128)(2,1)} %x_h.1, ...), custom_call_target="tpu_custom_call" | custom-call | tf_op jit(solution)/shard_map/mid/pallas_call | solution.py:588
  553.0 33.7 %last.1 = (bf16[4096,1024]{1,0:T(8,128)(2,1)}, bf16[4096,1024]{1,0:T(8,128)(2,1)}, bf16[1024,4096]{1,0:T(8,128)(2,1)}, bf16[4096,1024]{1,0:T(8,128)(2,1)}, bf16[...) custom-call(bf16[4096,1024]{1,0:T(8,128)(2,1)} %get-tuple-element.29, ...), custom_call_target="tpu_custom_call" | custom-call | tf_op jit(solution)/shard_map/last/pallas_call | solution.py:639
